TPU v7x, 32 devices: a whole 2x2x4 slice. The times are simulated.
32 devices in a mesh: zero: 8 (over y, x, core), tp: 4 (over z).
Axes of the slice: x: 2, y: 2, z: 4, core: 2. Of those that a mesh axis runs over, the one named last changes fastest.
Arguments:
- weight_gate: bfloat16 [2560, 9728], P('zero', 'tp'), may hold values from -0.125 to 0.125
- low_gate: bfloat16 [2560, 16], P('zero'), may hold values from -0.125 to 0.125
- high_gate: bfloat16 [16, 9728], P(None, 'tp'), may hold values from -1.5 to 1.5
- weight_up: bfloat16 [2560, 9728], P('zero', 'tp'), may hold values from -0.125 to 0.125
- low_up: bfloat16 [2560, 16], P('zero'), may hold values from -0.125 to 0.125
- high_up: bfloat16 [16, 9728], P(None, 'tp'), may hold values from -1.5 to 1.5
- weight_down: bfloat16 [9728, 2560], P('tp', 'zero'), may hold values from -0.0625 to 0.0625
- low_down: bfloat16 [9728, 16], P('tp'), may hold values from -0.0625 to 0.0625
- high_down: bfloat16 [16, 2560], P(None, 'zero'), may hold values from -1.5 to 1.5
- norm_train: float32 [2560], P(('zero', 'tp')), may hold values from 0.25 to 1.75
- norm_step: float32 [2560], P(('zero', 'tp')), may hold values from -0.3 to 0.3
Outputs:
- ready_gate: bfloat16 [2560, 9728], P(None, 'tp')
- ready_up: bfloat16 [2560, 9728], P(None, 'tp')
- ready_down: bfloat16 [9728, 2560], P('tp')
- serve_norm: bfloat16 [2560], replicated
All inputs are finite; a program needn't handle non-finite values.
Results may differ from a plain program's by a relative error of at most 0.001.
Values may be sent and summed in bfloat16 or wider, within the bound.
A program may use at most 128 MiB of HBM per device.

v0:
```python
import jax
import jax.numpy as jnp
from jax import lax
from jax.sharding import PartitionSpec as P

mix_rate = 0.5


def local(
    weight_gate,
    low_gate,
    high_gate,
    weight_up,
    low_up,
    high_up,
    weight_down,
    low_down,
    high_down,
    norm_train,
    norm_step,
):
    moved_gate, moved_up, moved_down, factor_gate, factor_up, factor_down = (
        lax.all_gather(weight_gate, "zero", axis=0, tiled=True),
        lax.all_gather(weight_up, "zero", axis=0, tiled=True),
        lax.all_gather(weight_down, "zero", axis=1, tiled=True),
        lax.all_gather(low_gate, "zero", axis=0, tiled=True),
        lax.all_gather(low_up, "zero", axis=0, tiled=True),
        lax.all_gather(high_down, "zero", axis=1, tiled=True),
    )
    latest_gate = moved_gate.astype(jnp.float32) + mix_rate * jnp.dot(
        factor_gate, high_gate, preferred_element_type=jnp.float32
    )
    ready_gate = latest_gate.astype(jnp.bfloat16)
    latest_up = moved_up.astype(jnp.float32) + mix_rate * jnp.dot(
        factor_up, high_up, preferred_element_type=jnp.float32
    )
    ready_up = latest_up.astype(jnp.bfloat16)
    latest_down = moved_down.astype(jnp.float32) + mix_rate * jnp.dot(
        low_down, factor_down, preferred_element_type=jnp.float32
    )
    ready_down = latest_down.astype(jnp.bfloat16)
    serve_norm = lax.all_gather(
        (norm_train + norm_step).astype(jnp.bfloat16), ("zero", "tp"), axis=0, tiled=True
    )
    return (ready_gate, ready_up, ready_down, serve_norm)


def solution(mesh):
    return jax.shard_map(
        local,
        mesh=mesh,
        in_specs=(
            P("zero", "tp"),
            P("zero", None),
            P(None, "tp"),
            P("zero", "tp"),
            P("zero", None),
            P(None, "tp"),
            P("tp", "zero"),
            P("tp", None),
            P(None, "zero"),
            P(("zero", "tp")),
            P(("zero", "tp")),
        ),
        out_specs=(P(None, "tp"), P(None, "tp"), P("tp", None), P()),
        check_vma=False,
    )
```

profile of v0, /device:TPU:0, one launch (start us, length us, event | category | flops | bytes accessed | tf_op | source)
XLA Modules:
  0.0 248.3 jit_solution(13862826156925674627)
XLA Ops:
  7.2 0.0 copy-start
  7.2 0.0 all-gather.11.cloned.1.call-start
  7.2 0.7 all-gather.11.cloned.1.call-update
  7.9 0.0 all-gather.7.cloned.1.call-start
  8.0 0.7 all-gather.7.cloned.1.call-update
  8.7 0.0 all-gather.9.cloned.1.call-start
  8.7 0.7 all-gather.9.cloned.1.call-update
  9.4 10.9 %all-gather = bf16[8,320,16]{1,2,0:T(8,128)(2,1)S(1)} all-gather(bf16[1,320,16]{1,2,0:T(8,128)(2,1)} %bitcast.17), channel_id=1, replica_groups=mesh['zero'=8,'tp'=4] {'zero'}, dimensions={0}, use_global_device_ids=true | all-gather | bytes 92160 | tf_op jit(solution)/shard_map/all_gather | solution.py:26
  20.3 0.1 reshape.11
  20.4 9.6 %all-gather.1 = bf16[8,320,16]{1,2,0:T(8,128)(2,1)S(1)} all-gather(bf16[1,320,16]{1,2,0:T(8,128)(2,1)} %bitcast.18), channel_id=1, replica_groups=mesh['zero'=8,'tp'=4] {'zero'}, dimensions={0}, use_global_device_ids=true | all-gather | bytes 92160 | tf_op jit(solution)/shard_map/all_gather | solution.py:27
  30.0 0.1 reshape.13
  30.1 9.0 %all-gather.2 = bf16[8,320,16]{1,2,0:T(8,128)(2,1)S(1)} all-gather(bf16[1,320,16]{1,2,0:T(8,128)(2,1)} %bitcast.19), channel_id=1, replica_groups=mesh['zero'=8,'tp'=4] {'zero'}, dimensions={0}, use_global_device_ids=true | all-gather | bytes 92160 | tf_op jit(solution)/shard_map/all_gather | solution.py:28
  39.2 0.1 reshape.15
  39.3 0.7 add_convert_fusion.3
  40.0 0.2 dynamic-update-slice
  40.2 40.8 %all-reduce = bf16[2560]{0:T(1024)(128)(2,1)} all-reduce(bf16[2560]{0:T(1024)(128)(2,1)S(1)} %dynamic-update-slice), channel_id=1, replica_groups=mesh['zero'=8,'tp'=4] {'zero','tp'}, use_global_device_ids=true, to_apply=%add | all-reduce | flops 2560 | bytes 10240
  81.0 4.8 %all-gather.11.cloned.1.call-done = bf16[2432,2560]{0,1:T(8,128)(2,1)} async-done(((bf16[2432,320]{0,1:T(8,128)(2,1)}), bf16[2432,2560]{0,1:T(8,128)(2,1)}) %all-gather.11.cloned.1.call-update) | async-done | bytes 12451856 | tf_op jit(solution)/shard_map/all_gather | solution.py:25
  85.8 17.3 %copy.22 = bf16[2432,2560]{1,0:T(8,128)(2,1)} copy(bf16[2432,2560]{0,1:T(8,128)(2,1)} %all-gather.11.cloned.1.call-done) | data formatting | bytes 24903680 | tf_op jit(solution)/shard_map/all_gather | solution.py:25
  103.0 0.0 copy-done
  103.0 9.4 %add_convert_fusion = bf16[2432,2560]{1,0:T(8,128)(2,1)} fusion(bf16[2432,2560]{1,0:T(8,128)(2,1)} %copy.22, bf16[2432,16]{0,1:T(8,128)(2,1)S(1)} %copy-done, bf16[2560,16]{0,1:T(8,128)(2,1)S(1)} %reshape.15), kind=kOutput, calls=%fused_computation | convolution fusion | flops 224133120 | bytes 25063424 | tf_op jit(solution)/shard_map/dot_general | solution.py:38
  112.4 46.7 %all-gather.7.cloned.1.call-done = bf16[2560,2432]{1,0:T(8,128)(2,1)} async-done(((bf16[320,2432]{1,0:T(8,128)(2,1)}), bf16[2560,2432]{1,0:T(8,128)(2,1)}) %all-gather.7.cloned.1.call-update) | async-done | bytes 12451856 | tf_op jit(solution)/shard_map/all_gather | solution.py:23
  159.1 9.4 %add_convert_fusion.2 = bf16[2560,2432]{1,0:T(8,128)(2,1)} fusion(bf16[2560,2432]{1,0:T(8,128)(2,1)} %all-gather.7.cloned.1.call-done, bf16[2560,16]{0,1:T(8,128)(2,1)S(1)} %reshape.11, bf16[16,2432]{1,0:T(8,128)(2,1)S(1)} %copy-done.2), kind=kOutput, calls=%fused_computation.2 | convolution fusion | flops 224133120 | bytes 25063424 | tf_op jit(solution)/shard_map/dot_general | solution.py:30
  168.4 64.0 %all-gather.9.cloned.1.call-done = bf16[2560,2432]{1,0:T(8,128)(2,1)} async-done(((bf16[320,2432]{1,0:T(8,128)(2,1)}), bf16[2560,2432]{1,0:T(8,128)(2,1)}) %all-gather.9.cloned.1.call-update) | async-done | bytes 12451856 | tf_op jit(solution)/shard_map/all_gather | solution.py:24
  232.4 9.3 %add_convert_fusion.1 = bf16[2560,2432]{1,0:T(8,128)(2,1)} fusion(bf16[2560,2432]{1,0:T(8,128)(2,1)} %all-gather.9.cloned.1.call-done, bf16[2560,16]{0,1:T(8,128)(2,1)S(1)} %reshape.13, bf16[16,2432]{1,0:T(8,128)(2,1)S(1)} %copy-done.3), kind=kOutput, calls=%fused_computation.1 | convolution fusion | flops 224133120 | bytes 25063424 | tf_op jit(solution)/shard_map/dot_general | solution.py:34
  (10 shorter events, 0.1 us)
Async XLA Ops:
  7.2 95.9 %copy-start = (bf16[2432,16]{0,1:T(8,128)(2,1)S(1)}, bf16[2432,16]{0,1:T(8,128)(2,1)}, u32[]{:S(2)}) copy-start(bf16[2432,16]{0,1:T(8,128)(2,1)} %param.18) | copy-start | bytes 233476
  7.2 78.6 %all-gather.11.cloned.1.call-start = ((), (), s32[]{:S(2)}) async-start(), calls=%async_computation.2 | async-start | bytes 14008320 | tf_op jit(solution)/shard_map/all_gather | solution.py:25
  7.9 151.1 %all-gather.7.cloned.1.call-start = ((), (), s32[]{:S(2)}) async-start(), calls=%async_computation | async-start | bytes 14008320 | tf_op jit(solution)/shard_map/all_gather | solution.py:23
  8.7 223.8 %all-gather.9.cloned.1.call-start = ((), (), s32[]{:S(2)}) async-start(), calls=%async_computation.1 | async-start | bytes 14008320 | tf_op jit(solution)/shard_map/all_gather | solution.py:24
  103.0 56.0 %copy-start.2 = (bf16[16,2432]{1,0:T(8,128)(2,1)S(1)}, bf16[16,2432]{1,0:T(8,128)(2,1)}, u32[]{:S(2)}) copy-start(bf16[16,2432]{1,0:T(8,128)(2,1)} %param.13) | copy-start | bytes 233476
  112.4 120.0 %copy-start.3 = (bf16[16,2432]{1,0:T(8,128)(2,1)S(1)}, bf16[16,2432]{1,0:T(8,128)(2,1)}, u32[]{:S(2)}) copy-start(bf16[16,2432]{1,0:T(8,128)(2,1)} %param.16) | copy-start | bytes 233476
  159.1 82.7 %copy-start.1 = (bf16[2432,16]{0,1:T(8,128)(2,1)S(1)}, bf16[2432,16]{0,1:T(8,128)(2,1)}, u32[]{:S(2)}) copy-start(bf16[2432,16]{0,1:T(8,128)(2,1)} %param.18) | copy-start | bytes 233476
Sparse Core Ops, SparseCore 0:
  9.9 75.8 all-gather.10
  87.6 71.3 all-gather.6
  161.0 71.4 all-gather.8
where the time goes:
time: 249 us; the launch traced here: 248 us
  waiting for transfers between devices  117 us (47%)
  blocking collectives  70.3 us (28%)
  matrix products  28.1 us (11%)
  local copies, waits for them, and re-layouts  17.9 us (7%)
  between operations  13.8 us (6%)
    all_gather x1, waiting for transfers between devices, local(): lax.all_gather(weight_up, 'zero', axis=0, tiled=True)  64 us
    all_gather x1, waiting for transfers between devices, local(): lax.all_gather(weight_gate, 'zero', axis=0, tiled=True)  46.7 us
    unnamed x1, blocking collectives  40.8 us
    all_gather x1, local copies, waits for them, and re-layouts, local(): lax.all_gather(weight_down, 'zero', axis=1, tiled=True)  17.3 us
    all_gather x1, blocking collectives, local(): lax.all_gather(low_gate, 'zero', axis=0, tiled=True)  10.9 us
    all_gather x1, blocking collectives, local(): lax.all_gather(low_up, 'zero', axis=0, tiled=True)  9.56 us
    dot_general x1, matrix products, local(): jnp.dot(low_down, factor_down, preferred_element_type=jnp.float32)  9.37 us
    dot_general x1, matrix products, local(): jnp.dot(factor_gate, high_gate, preferred_element_type=jnp.float32)  9.36 us
  transfers between devices with their start and end apart: 3, of which 3 were waited for; matrix products, arithmetic and copies ran while one was open for 15% of the time, Pallas kernels for 0%

commit v1 on v0

--- a/solution.py
+++ b/solution.py
@@ -4,6 +4,11 @@
 from jax.sharding import PartitionSpec as P
 
 mix_rate = 0.5
+
+
+def _move_quotas(array_in):
+    v_now = lax.all_gather(array_in, "zero")
+    return jnp.concatenate(v_now, axis=1)
 
 
 def local(
@@ -22,7 +27,7 @@
     moved_gate, moved_up, moved_down, factor_gate, factor_up, factor_down = (
         lax.all_gather(weight_gate, "zero", axis=0, tiled=True),
         lax.all_gather(weight_up, "zero", axis=0, tiled=True),
-        lax.all_gather(weight_down, "zero", axis=1, tiled=True),
+        _move_quotas(weight_down),
         lax.all_gather(low_gate, "zero", axis=0, tiled=True),
         lax.all_gather(low_up, "zero", axis=0, tiled=True),
         lax.all_gather(high_down, "zero", axis=1, tiled=True),

time: 249 us -> 249 us (level)
  waiting for transfers between devices: 117 us -> 62.6 us
  local copies, waits for them, and re-layouts: 17.9 us -> 59.8 us
  other arithmetic: 0.68 us -> 7.72 us
  matrix products: 28.1 us -> 33.9 us
    all_gather x1, waiting for transfers between devices: 64 us -> 7.09 us  [local(): lax.all_gather(weight_up, 'zero', axis=0, tiled=True)]
    convert_element_type x0 -> x2, local copies, waits for them, and re-layouts: none -> 49.2 us  [local(): moved_down.astype(jnp.float32)]
    all_gather x1 -> x0, local copies, waits for them, and re-layouts: 17.3 us -> none  [local(): lax.all_gather(weight_down, 'zero', axis=1, tiled=True)]
    unnamed x13 -> x12, local copies, waits for them, and re-layouts: 0.59 us -> 10.6 us
    convert_element_type x0 -> x1, other arithmetic: none -> 7.04 us  [local(): moved_down.astype(jnp.float32)]
    dot_general x1, matrix products: 9.37 us -> 15.3 us  [local(): jnp.dot(low_down, factor_down, preferred_element_type=jnp.float32)]
  transfers between devices with their start and end apart: 3 -> 3, of which waited for: 3 -> 3; matrix products, arithmetic and copies ran while one was open for 15% -> 37% of each run, Pallas kernels for 0% -> 0%
where the time goes in v1:
time: 249 us; the launch traced here: 248 us
  blocking collectives  70.3 us (28%)
  waiting for transfers between devices  62.6 us (25%)
  local copies, waits for them, and re-layouts  59.8 us (24%)
  matrix products  33.9 us (14%)
  between operations  13.8 us (6%)
  other arithmetic  7.72 us (3%)
    convert_element_type x2, local copies, waits for them, and re-layouts, local(): moved_down.astype(jnp.float32)  49.2 us
    all_gather x1, waiting for transfers between devices, local(): lax.all_gather(weight_gate, 'zero', axis=0, tiled=True)  48.8 us
    unnamed x1, blocking collectives  40.8 us
    dot_general x1, matrix products, local(): jnp.dot(low_down, factor_down, preferred_element_type=jnp.float32)  15.3 us
    all_gather x1, blocking collectives, local(): lax.all_gather(high_down, 'zero', axis=1, tiled=True)  10.9 us
    unnamed x12, local copies, waits for them, and re-layouts  10.6 us
    all_gather x1, blocking collectives, local(): lax.all_gather(low_up, 'zero', axis=0, tiled=True)  9.56 us
    dot_general x1, matrix products, local(): jnp.dot(factor_up, high_up, preferred_element_type=jnp.float32)  9.33 us
  transfers between devices with their start and end apart: 3, of which 3 were waited for; matrix products, arithmetic and copies ran while one was open for 37% of the time, Pallas kernels for 0%

profile of v1, /device:TPU:0, one launch (start us, length us, event | category | flops | bytes accessed | tf_op | source)
XLA Modules:
  0.0 248.2 jit_solution(7973017726759519328)
XLA Ops:
  7.2 0.7 all-gather.12.cloned.1.call-update
  7.9 0.0 all-gather.10.cloned.1.call-start
  8.0 0.7 all-gather.10.cloned.1.call-update
  8.7 0.0 all-gather.8.cloned.1.call-start
  8.7 0.7 all-gather.8.cloned.1.call-update
  9.4 10.9 %all-gather.3 = bf16[8,320,16]{1,2,0:T(8,128)(2,1)S(1)} all-gather(bf16[1,320,16]{1,2,0:T(8,128)(2,1)} %bitcast.27), channel_id=1, replica_groups=mesh['zero'=8,'tp'=4] {'zero'}, dimensions={0}, use_global_device_ids=true | all-gather | bytes 92160 | tf_op jit(solution)/shard_map/all_gather | solution.py:33
  20.3 0.1 reshape.22
  20.4 9.6 %all-gather.2 = bf16[8,320,16]{1,2,0:T(8,128)(2,1)S(1)} all-gather(bf16[1,320,16]{1,2,0:T(8,128)(2,1)} %bitcast.28), channel_id=1, replica_groups=mesh['zero'=8,'tp'=4] {'zero'}, dimensions={0}, use_global_device_ids=true | all-gather | bytes 92160 | tf_op jit(solution)/shard_map/all_gather | solution.py:32
  30.0 0.1 reshape.20
  30.1 9.0 %all-gather.1 = bf16[8,320,16]{1,2,0:T(8,128)(2,1)S(1)} all-gather(bf16[1,320,16]{1,2,0:T(8,128)(2,1)} %bitcast.29), channel_id=1, replica_groups=mesh['zero'=8,'tp'=4] {'zero'}, dimensions={0}, use_global_device_ids=true | all-gather | bytes 92160 | tf_op jit(solution)/shard_map/all_gather | solution.py:31
  39.2 0.1 reshape.18
  39.3 0.7 add_convert_fusion.3
  40.0 0.2 dynamic-update-slice
  40.2 40.8 %all-reduce = bf16[2560]{0:T(1024)(128)(2,1)} all-reduce(bf16[2560]{0:T(1024)(128)(2,1)S(1)} %dynamic-update-slice), channel_id=1, replica_groups=mesh['zero'=8,'tp'=4] {'zero','tp'}, use_global_device_ids=true, to_apply=%add | all-reduce | flops 2560 | bytes 10240
  81.0 4.6 %all-gather.12.cloned.1.call-done = bf16[19456,320]{0,1:T(8,128)(2,1)} async-done(((bf16[2432,320]{0,1:T(8,128)(2,1)}), bf16[19456,320]{0,1:T(8,128)(2,1)}) %all-gather.12.cloned.1.call-update) | async-done | bytes 12451856 | tf_op jit(solution)/shard_map/all_gather | solution.py:10
  85.7 7.0 %convert_element_type.38 = f32[19456,320]{0,1:T(8,128)S(1)} convert(bf16[19456,320]{0,1:T(8,128)(2,1)} %all-gather.12.cloned.1.call-done) | non-fusion elementwise | flops 6225920 | bytes 37355520 | tf_op jit(solution)/shard_map/convert_element_type | solution.py:43
  92.7 10.0 %copy.30 = f32[40,8,8,2432]{3,2,1,0:T(8,128)} copy(f32[40,8,8,2432]{3,1,2,0:T(8,128)S(1)} %bitcast.24) | data formatting | bytes 49807360
  102.7 22.2 %copy.27 = f32[2432,8,320]{0,2,1:T(8,128)} copy(f32[2432,8,320]{0,1,2:T(8,128)} %bitcast.25) | data formatting | bytes 49807360 | tf_op jit(solution)/shard_map/convert_element_type | solution.py:43
  125.0 26.9 %copy.29 = f32[2432,2560]{1,0:T(8,128)} copy(f32[2432,2560]{0,1:T(8,128)} %bitcast.26) | data formatting | bytes 49807360 | tf_op jit(solution)/shard_map/convert_element_type | solution.py:43
  151.9 7.1 %all-gather.10.cloned.1.call-done = bf16[2560,2432]{1,0:T(8,128)(2,1)} async-done(((bf16[320,2432]{1,0:T(8,128)(2,1)}), bf16[2560,2432]{1,0:T(8,128)(2,1)}) %all-gather.10.cloned.1.call-update) | async-done | bytes 12451856 | tf_op jit(solution)/shard_map/all_gather | solution.py:29
  159.0 9.3 %add_convert_fusion.1 = bf16[2560,2432]{1,0:T(8,128)(2,1)} fusion(bf16[2560,2432]{1,0:T(8,128)(2,1)} %all-gather.10.cloned.1.call-done, bf16[2560,16]{0,1:T(8,128)(2,1)S(1)} %reshape.20, bf16[16,2432]{1,0:T(8,128)(2,1)S(1)} %copy-done), kind=kOutput, calls=%fused_computation.1 | convolution fusion | flops 224133120 | bytes 25063424 | tf_op jit(solution)/shard_map/dot_general | solution.py:39
  168.3 15.3 %add_convert_fusion = bf16[2432,2560]{1,0:T(8,128)(2,1)} fusion(f32[2432,2560]{1,0:T(8,128)} %copy.29, bf16[2432,16]{0,1:T(8,128)(2,1)S(1)} %copy-done.1, bf16[2560,16]{0,1:T(8,128)(2,1)S(1)} %reshape.22), kind=kOutput, calls=%fused_computation | convolution fusion | flops 217907200 | bytes 37515264 | tf_op jit(solution)/shard_map/dot_general | solution.py:43
  183.6 48.8 %all-gather.8.cloned.1.call-done = bf16[2560,2432]{1,0:T(8,128)(2,1)} async-done(((bf16[320,2432]{1,0:T(8,128)(2,1)}), bf16[2560,2432]{1,0:T(8,128)(2,1)}) %all-gather.8.cloned.1.call-update) | async-done | bytes 12451856 | tf_op jit(solution)/shard_map/all_gather | solution.py:28
  232.3 9.3 %add_convert_fusion.2 = bf16[2560,2432]{1,0:T(8,128)(2,1)} fusion(bf16[2560,2432]{1,0:T(8,128)(2,1)} %all-gather.8.cloned.1.call-done, bf16[2560,16]{0,1:T(8,128)(2,1)S(1)} %reshape.18, bf16[16,2432]{1,0:T(8,128)(2,1)S(1)} %copy-done.2), kind=kOutput, calls=%fused_computation.2 | convolution fusion | flops 224133120 | bytes 25063424 | tf_op jit(solution)/shard_map/dot_general | solution.py:35
  (11 shorter events, 0.1 us)
Async XLA Ops:
  7.2 151.8 %copy-start = (bf16[16,2432]{1,0:T(8,128)(2,1)S(1)}, bf16[16,2432]{1,0:T(8,128)(2,1)}, u32[]{:S(2)}) copy-start(bf16[16,2432]{1,0:T(8,128)(2,1)} %param.16) | copy-start | bytes 233476
  7.2 78.5 %all-gather.12.cloned.1.call-start = ((), (), s32[]{:S(2)}) async-start(), calls=%async_computation.2 | async-start | bytes 14008320 | tf_op jit(solution)/shard_map/all_gather | solution.py:10
  7.9 151.1 %all-gather.10.cloned.1.call-start = ((), (), s32[]{:S(2)}) async-start(), calls=%async_computation.1 | async-start | bytes 14008320 | tf_op jit(solution)/shard_map/all_gather | solution.py:29
  8.7 223.7 %all-gather.8.cloned.1.call-start = ((), (), s32[]{:S(2)}) async-start(), calls=%async_computation | async-start | bytes 14008320 | tf_op jit(solution)/shard_map/all_gather | solution.py:28
  151.9 16.4 %copy-start.1 = (bf16[2432,16]{0,1:T(8,128)(2,1)S(1)}, bf16[2432,16]{0,1:T(8,128)(2,1)}, u32[]{:S(2)}) copy-start(bf16[2432,16]{0,1:T(8,128)(2,1)} %param.18) | copy-start | bytes 233476
  168.3 64.0 %copy-start.2 = (bf16[16,2432]{1,0:T(8,128)(2,1)S(1)}, bf16[16,2432]{1,0:T(8,128)(2,1)}, u32[]{:S(2)}) copy-start(bf16[16,2432]{1,0:T(8,128)(2,1)} %param.13) | copy-start | bytes 233476
Sparse Core Ops, SparseCore 0:
  9.9 75.7 all-gather.11
  87.6 71.3 all-gather.9
  160.9 71.4 all-gather.7
